TPU v7x, 32 devices: a whole 2x2x4 slice. The times are simulated.
32 devices in a mesh: tm: 16 (over z, y, x), state: 2 (over core).
Axes of the slice: x: 2, y: 2, z: 4, core: 2. Of those that a mesh axis runs over, the one named last changes fastest.
Arguments:
- symbols: int32 [8], P('state'), may hold values from 0 to 255
- emission: float32 [8192, 256], P('tm'), may hold values from 0.2 to 5
- decay: float32 [2, 8192], P('state', 'tm'), may hold values from 0.05 to 1
- left_factor: float32 [2, 64, 8192], P('state', None, 'tm'), may hold values from 0.1 to 3
- right_factor: float32 [2, 64, 8192], P('state', None, 'tm'), may hold values from 0.001 to 0.03
- initial: float32 [8192], P('tm'), may hold values from 0.1 to 10
Outputs:
- filtered: float32 [8, 8192], P('state', 'tm')
- log_scale: float32 [8], P('state')
All inputs are finite; a program needn't handle non-finite values.
Results may differ from a plain program's by a relative error of at most 0.00011.
Values sent between devices are 32-bit elements; how exact they have to be, the bound alone decides.
No kernel may reach another device: no remote copies, remote signals or barrier semaphores. Data moves between devices by JAX's collectives and lax.ppermute only.
A program may use at most 64 MiB of HBM per device.

v0:
```python
import jax
import jax.numpy as jnp
from jax import lax
from jax.sharding import PartitionSpec as P

S = 8192
PRECISE = lax.Precision.HIGHEST


def passed_along(value, axis, steps):
    count = lax.axis_size(axis)
    first, last = (max(0, -steps), min(count, count - steps))
    return lax.ppermute(value, axis, [(source, source + steps) for source in range(first, last)])


def run_span(entry_vec, emitted_all, decay_row, left_rows, right_rows):
    projected, total_sum = lax.psum(
        (jnp.dot(left_rows, entry_vec, precision=PRECISE), jnp.sum(entry_vec)), "tm"
    )
    rescale = S / total_sum
    belief = entry_vec * rescale
    mixture = projected * rescale / S

    def frame(state_pair, emitted):
        belief_now, mixture_now = state_pair
        unscaled = emitted * (
            decay_row * belief_now + jnp.dot(mixture_now, right_rows, precision=PRECISE)
        )
        proj_next, total_next = lax.psum(
            (jnp.dot(left_rows, unscaled, precision=PRECISE), jnp.sum(unscaled)), "tm"
        )
        normal = total_next / S
        belief_next = unscaled / normal
        mixture_next = proj_next / normal / S
        return ((belief_next, mixture_next), (belief_next, jnp.log(normal)))

    (closing, mixture_end), (beliefs, log_levels) = lax.scan(frame, (belief, mixture), emitted_all)
    return (beliefs, log_levels, closing)


def span_map(emitted_all, decay_row, left_rows, right_rows):
    frames = emitted_all.shape[0]
    rank_cols = left_rows.shape[0]
    cells = left_rows.shape[1]
    growth = emitted_all * decay_row[None, :]
    markers = jnp.eye(frames, dtype=jnp.float32)

    def advance(state_pair, inputs):
        reached, weights = state_pair
        grow_row, emitted, marker = inputs
        weights_next = weights * grow_row[None, :] + marker[:, None] * emitted[None, :]
        return ((reached * grow_row, weights_next), (reached, weights_next))

    begin_pair = (jnp.ones((cells,), jnp.float32), jnp.zeros((frames, cells), jnp.float32))
    (final_reach, final_weights), (reached_all, weights_all) = lax.scan(
        advance, begin_pair, (growth, emitted_all, markers)
    )
    probes = (left_rows[None, :, :] * reached_all[:, None, :]).reshape(
        frames * rank_cols, cells
    ) / S
    vb_rows = right_rows[None, :, :] * final_weights[:, None, :]
    pair_rows = weights_all[: frames - 1].reshape((frames - 1) * frames, cells)
    group_size = max(rank_cols // 8, 1)
    blocks = []
    for offset in range(0, rank_cols, group_size):
        cross_rows = (
            left_rows[offset : offset + group_size, None, :] * right_rows[None, :, :]
        ).reshape(-1, cells)
        blocks.append(jnp.einsum("pw,qw->pq", pair_rows, cross_rows, precision=PRECISE))
    local_terms = jnp.concatenate(blocks, axis=1) / S
    coupling = lax.psum(local_terms, "tm").reshape(frames - 1, frames, rank_cols, rank_cols)
    shifted = jnp.concatenate(
        [jnp.zeros((1, frames, rank_cols, rank_cols), jnp.float32), coupling], axis=0
    )

    def solve_back(turn_index, response):
        column = frames - 1 - turn_index
        factors = lax.dynamic_index_in_dim(shifted, column, 1, keepdims=False)
        coupled = jnp.einsum("kab,kaw->bw", factors, response, precision=PRECISE)
        own_rows = lax.dynamic_index_in_dim(vb_rows, column, 0, keepdims=False)
        return lax.dynamic_update_index_in_dim(response, own_rows + coupled, column, 0)

    response = lax.fori_loop(
        0, frames, solve_back, jnp.zeros((frames, rank_cols, cells), jnp.float32)
    )
    return (probes, final_reach, response)


def per_device(symbols, emission, decay, left_factor, right_factor, initial):
    decay_row = decay[0]
    left_rows = left_factor[0]
    right_rows = right_factor[0]
    onehot = (symbols[:, None] == jnp.arange(emission.shape[1], dtype=jnp.int32)[None, :]).astype(
        jnp.float32
    )
    emitted_all = jnp.einsum("fv,sv->fs", onehot, emission, precision=PRECISE)
    leader = lax.axis_index("state") == 0

    def pass_on(closing):
        return jnp.where(leader, initial, passed_along(closing, "state", 1))

    probes, final_reach, response = span_map(emitted_all, decay_row, left_rows, right_rows)
    frames = emitted_all.shape[0]
    rank_cols = left_rows.shape[0]

    def section(step_idx, entry_vec):
        projected, total_sum = lax.psum(
            (jnp.dot(probes, entry_vec, precision=PRECISE), jnp.sum(entry_vec)), "tm"
        )
        rescale = S / total_sum
        carried = jnp.einsum(
            "ka,kaw->w",
            (projected * rescale).reshape(frames, rank_cols),
            response,
            precision=PRECISE,
        )
        return pass_on(final_reach * entry_vec * rescale + carried)

    entry_vec = lax.fori_loop(0, lax.axis_size("state") - 1, section, initial)
    beliefs, log_levels, closing = run_span(
        entry_vec, emitted_all, decay_row, left_rows, right_rows
    )
    return (beliefs, log_levels)


def solution(mesh):
    return jax.shard_map(
        per_device,
        mesh=mesh,
        in_specs=(
            P("state"),
            P("tm", None),
            P("state", "tm"),
            P("state", None, "tm"),
            P("state", None, "tm"),
            P("tm"),
        ),
        out_specs=(P("state", "tm"), P("state")),
        check_vma=False,
    )
```

profile of v0, /device:TPU:0, one launch (start us, length us, event | category | flops | bytes accessed | tf_op | source)
XLA Modules:
  0.0 347.2 jit_solution(12387997942848952314)
XLA Ops:
  7.3 0.9 slice_bitcast_fusion
  8.3 0.6 copy-done.3
  8.9 0.4 broadcast_multiply_fusion.10
  9.3 0.8 while.54
  10.2 1.1 broadcast_multiply_fusion
  11.3 1.0 convolution_dynamic-update-slice_fusion.7
  12.2 1.0 convolution_dynamic-update-slice_fusion.6
  13.2 1.0 convolution_dynamic-update-slice_fusion.5
  14.2 1.0 convolution_dynamic-update-slice_fusion.4
  15.2 1.0 convolution_dynamic-update-slice_fusion.3
  16.1 1.0 convolution_dynamic-update-slice_fusion.2
  17.1 1.0 convolution_dynamic-update-slice_fusion.1
  18.1 1.0 convolution_dynamic-update-slice_fusion
  19.3 0.9 copy.8
  20.2 0.9 copy-done.1
  21.2 0.6 copy-done.4
  21.8 0.6 reduce_sum.28
  22.4 0.5 fusion.17
  22.9 44.2 %all-reduce.3 = (f32[256]{0:T(256)S(1)}, f32[]{:T(128)}) all-reduce(f32[256]{0:T(256)S(1)} %bitcast.161, f32[]{:T(128)} %reduce_sum.28), channel_id=1, replica_groups=mesh['tm'=16,'state'=2] {'tm'}, use_global_device_ids=true, to_apply=%region_4.5 | all-reduce | flops 257 | bytes 2056 | tf_op jit(solution)/shard_map/while/body/eval_jaxpr/psum | solution.py:107
  67.9 63.9 %all-reduce.8.cloned.1.call-done = f32[3,4,64,64]{2,3,0,1:T(8,128)} async-done(((f32[3,4,64,64]{2,3,0,1:T(8,128)}), f32[3,4,64,64]{2,3,0,1:T(8,128)}) %all-reduce.8.cloned.1.call-update) | async-done | bytes 196624 | tf_op jit(solution)/shard_map/psum | solution.py:71
  131.8 1.0 concatenate.7
  132.9 2.0 while.52
  133.0 0.5 fusion.58
  133.4 0.4 fusion.58
  133.9 0.5 fusion.58
  134.4 0.4 fusion.58
  134.9 0.4 fusion.18
  135.3 1.3 collective-permute-start
  136.6 0.8 collective-permute-done
  137.4 0.6 fusion.16
  138.0 0.2 convolution_bitcast_fusion.2
  138.2 40.5 %all-reduce.2 = (f32[]{:T(128)}, f32[64]{0:T(128)S(1)}) all-reduce(f32[]{:T(128)} %get-tuple-element.314, f32[64]{0:T(128)S(1)} %convolution_bitcast_fusion.2), channel_id=1, replica_groups=mesh['tm'=16,'state'=2] {'tm'}, use_global_device_ids=true, to_apply=%region_9.10 | all-reduce | flops 65 | bytes 520 | tf_op jit(solution)/shard_map/psum | solution.py:17
  179.4 160.4 %while.53 = (s32[]{:T(128)}, f32[512]{0:T(512)S(1)}, f32[64]{0:T(128)S(1)}, f32[4,512]{1,0:T(4,128)S(1)}, f32[4]{0:T(128)S(1)}, /*index=5*/f32[4,512]{1,0:T(4,12...) while((s32[]{:T(128)}, f32[512]{0:T(512)S(1)}, ...), condition=%wide.region_15.16_spmd, body=%wide.region_11.15_spmd.sunk | while | flops 789187 | bytes 290481 | solution.py:37
  179.4 0.2 fusion.63
  179.6 0.6 fusion.64
  180.2 0.2 convolution_bitcast_fusion.4
  180.4 37.2 %all-reduce.5 = (f32[]{:T(128)}, f32[64]{0:T(128)S(1)}) all-reduce(f32[]{:T(128)} %get-tuple-element.468, f32[64]{0:T(128)S(1)} %convolution_bitcast_fusion.4), channel_id=1, replica_groups=mesh['tm'=16,'state'=2] {'tm'}, use_global_device_ids=true, to_apply=%region_13.13 | all-reduce | flops 65 | bytes 520 | tf_op jit(solution)/shard_map/while/body/eval_jaxpr/psum | solution.py:29
  218.5 0.2 fusion.63
  218.7 0.6 fusion.64
  219.3 0.2 convolution_bitcast_fusion.4
  219.5 39.2 %all-reduce.5 = (f32[]{:T(128)}, f32[64]{0:T(128)S(1)}) all-reduce(f32[]{:T(128)} %get-tuple-element.468, f32[64]{0:T(128)S(1)} %convolution_bitcast_fusion.4), channel_id=1, replica_groups=mesh['tm'=16,'state'=2] {'tm'}, use_global_device_ids=true, to_apply=%region_13.13 | all-reduce | flops 65 | bytes 520 | tf_op jit(solution)/shard_map/while/body/eval_jaxpr/psum | solution.py:29
  259.6 0.2 fusion.63
  259.8 0.6 fusion.64
  260.5 37.3 %all-reduce.5 = (f32[]{:T(128)}, f32[64]{0:T(128)S(1)}) all-reduce(f32[]{:T(128)} %get-tuple-element.468, f32[64]{0:T(128)S(1)} %convolution_bitcast_fusion.4), channel_id=1, replica_groups=mesh['tm'=16,'state'=2] {'tm'}, use_global_device_ids=true, to_apply=%region_13.13 | all-reduce | flops 65 | bytes 520 | tf_op jit(solution)/shard_map/while/body/eval_jaxpr/psum | solution.py:29
  298.7 0.2 fusion.63
  298.9 0.6 fusion.64
  299.7 39.2 %all-reduce.5 = (f32[]{:T(128)}, f32[64]{0:T(128)S(1)}) all-reduce(f32[]{:T(128)} %get-tuple-element.468, f32[64]{0:T(128)S(1)} %convolution_bitcast_fusion.4), channel_id=1, replica_groups=mesh['tm'=16,'state'=2] {'tm'}, use_global_device_ids=true, to_apply=%region_13.13 | all-reduce | flops 65 | bytes 520 | tf_op jit(solution)/shard_map/while/body/eval_jaxpr/psum | solution.py:29
  339.8 0.5 copy-done.7
  (79 shorter events, 2.6 us)
Async XLA Ops:
  7.2 1.2 copy-start
  7.2 124.7 %all-reduce.8.cloned.1.call-start = ((), (), s32[]{:S(2)}) async-start(), calls=%async_computation | async-start | bytes 786432 | tf_op jit(solution)/shard_map/psum | solution.py:71
  8.2 0.7 copy-start.3
  8.2 0.7 copy-start.6
  9.2 0.9 copy-start.2
  20.2 0.9 copy-start.1
  21.1 0.7 copy-start.4
  135.3 2.1 collective-permute-start
  339.8 0.5 copy-start.7
  339.8 0.6 copy-start.5
Sparse Core Ops, SparseCore 0:
  20.3 111.4 all-reduce.7
where the time goes:
time: 348 us; the launch traced here: 347 us
  blocking collectives  238 us (68%)
  waiting for transfers between devices  64.7 us (19%)
  between operations  15.6 us (4%)
  matrix products  12.4 us (4%)
  local copies, waits for them, and re-layouts  7.07 us (2%)
  other arithmetic  5.31 us (2%)
    psum x4, blocking collectives, frame(): lax.psum((jnp.dot(left_rows, unscaled, precision=PRECISE), jnp.sum(unscal...  153 us
    psum x1, waiting for transfers between devices, span_map(): lax.psum(local_terms, 'tm')  63.9 us
    psum x1, blocking collectives, section(): lax.psum((jnp.dot(probes, entry_vec, precision=PRECISE), jnp.sum(entry_ve...  44.2 us
    psum x1, blocking collectives, run_span(): lax.psum((jnp.dot(left_rows, entry_vec, precision=PRECISE), jnp.sum(entry...  40.5 us
    dot_general x8, matrix products, span_map(): jnp.einsum('pw,qw->pq', pair_rows, cross_rows, precision=PRECISE)  7.79 us
  transfers between devices with their start and end apart: 2, of which 2 were waited for; matrix products, arithmetic and copies ran while one was open for 0% of the time, Pallas kernels for 0%

commit v1 on v0

--- a/solution.py
+++ b/solution.py
@@ -5,6 +5,12 @@
 
 S = 8192
 PRECISE = lax.Precision.HIGHEST
+
+
+def gather_and_add(x, axis):
+    parts = lax.all_gather(x, axis, axis=0, tiled=False)
+    total = parts.sum(axis=0)
+    return total
 
 
 def passed_along(value, axis, steps):
@@ -68,7 +74,7 @@
         ).reshape(-1, cells)
         blocks.append(jnp.einsum("pw,qw->pq", pair_rows, cross_rows, precision=PRECISE))
     local_terms = jnp.concatenate(blocks, axis=1) / S
-    coupling = lax.psum(local_terms, "tm").reshape(frames - 1, frames, rank_cols, rank_cols)
+    coupling = gather_and_add(local_terms, "tm").reshape(frames - 1, frames, rank_cols, rank_cols)
     shifted = jnp.concatenate(
         [jnp.zeros((1, frames, rank_cols, rank_cols), jnp.float32), coupling], axis=0
     )

time: 348 us -> 316 us (0.908)
  waiting for transfers between devices: 64.7 us -> 32.9 us
  other arithmetic: 5.31 us -> 9.34 us
  local copies, waits for them, and re-layouts: 7.07 us -> 3.04 us
    psum x1 -> x0, waiting for transfers between devices: 63.9 us -> none  [span_map(): lax.psum(local_terms, 'tm')]
    all_gather x0 -> x1, waiting for transfers between devices: none -> 32.1 us  [gather_and_add(): parts = lax.all_gather(x, axis, axis=0, tiled=False)]
where the time goes in v1:
time: 316 us
  blocking collectives  237 us (75%)
  waiting for transfers between devices  32.9 us (10%)
  between operations  15.6 us (5%)
  matrix products  12.9 us (4%)
  other arithmetic  9.34 us (3%)
  loops' own time  3.19 us (1%)
    psum x4, blocking collectives, frame(): lax.psum((jnp.dot(left_rows, unscaled, precision=PRECISE), jnp.sum(unscal...  153 us
    psum x1, blocking collectives, section(): lax.psum((jnp.dot(probes, entry_vec, precision=PRECISE), jnp.sum(entry_ve...  44.4 us
    psum x1, blocking collectives, run_span(): lax.psum((jnp.dot(left_rows, entry_vec, precision=PRECISE), jnp.sum(entry...  40.1 us
    all_gather x1, waiting for transfers between devices, gather_and_add(): parts = lax.all_gather(x, axis, axis=0, tiled=False)  32.1 us
    dot_general x8, matrix products, span_map(): jnp.einsum('pw,qw->pq', pair_rows, cross_rows, precision=PRECISE)  7.78 us
  transfers between devices with their start and end apart: 2, of which 2 were waited for; matrix products, arithmetic and copies ran while one was open for 0% of the time, Pallas kernels for 0%

profile of v1, /device:TPU:0, one launch (start us, length us, event | category | flops | bytes accessed | tf_op | source)
XLA Modules:
  0.0 315.7 jit_solution(13033362899725686888)
XLA Ops:
  7.3 0.9 slice_bitcast_fusion
  8.2 0.2 copy-done
  8.3 1.0 broadcast_multiply_fusion.10
  9.4 0.8 while.54
  10.2 2.0 broadcast_multiply_fusion
  12.2 1.0 fusion.16
  13.2 1.0 fusion.15
  14.2 1.0 fusion.14
  15.2 1.0 fusion.13
  16.1 1.0 fusion.12
  17.1 1.0 fusion.11
  18.1 1.0 fusion.10
  19.1 1.0 fusion.9
  20.0 0.7 broadcast_multiply_fusion.9
  20.8 0.6 reduce_sum.37
  21.5 0.5 fusion.25
  22.0 44.4 %all-reduce.3 = (f32[256]{0:T(256)S(1)}, f32[]{:T(128)}) all-reduce(f32[256]{0:T(256)S(1)} %bitcast.194, f32[]{:T(128)} %reduce_sum.37), channel_id=1, replica_groups=mesh['tm'=16,'state'=2] {'tm'}, use_global_device_ids=true, to_apply=%region_4.5 | all-reduce | flops 257 | bytes 2056 | tf_op jit(solution)/shard_map/while/body/eval_jaxpr/psum | solution.py:113
  67.2 32.1 %all-gather.2.cloned.1.call-done = f32[16,12,4096]{2,1,0:T(8,128)} async-done(((f32[1,12,4096]{2,1,0:T(8,128)}), f32[16,12,4096]{2,1,0:T(8,128)}) %all-gather.2.cloned.1.call-update) | async-done | bytes 3145744 | tf_op jit(solution)/shard_map/all_gather | solution.py:11
  99.2 2.4 reduce_sum.38
  102.0 1.8 while.52
  102.0 0.4 fusion.66
  102.4 0.4 fusion.66
  102.9 0.4 fusion.66
  103.3 0.4 fusion.66
  103.8 0.4 fusion.26
  104.1 1.3 collective-permute-start
  105.5 0.8 collective-permute-done
  106.2 0.6 fusion.24
  106.8 0.2 convolution_bitcast_fusion.10
  107.0 40.1 %all-reduce.2 = (f32[]{:T(128)}, f32[64]{0:T(128)S(1)}) all-reduce(f32[]{:T(128)} %get-tuple-element.322, f32[64]{0:T(128)S(1)} %convolution_bitcast_fusion.10), channel_id=1, replica_groups=mesh['tm'=16,'state'=2] {'tm'}, use_global_device_ids=true, to_apply=%region_9.10 | all-reduce | flops 65 | bytes 520 | tf_op jit(solution)/shard_map/psum | solution.py:23
  147.8 160.4 %while.53 = (s32[]{:T(128)}, f32[512]{0:T(512)S(1)}, f32[64]{0:T(128)S(1)}, f32[4,512]{1,0:T(4,128)S(1)}, f32[4]{0:T(128)S(1)}, /*index=5*/f32[4,512]{1,0:T(4,12...) while((s32[]{:T(128)}, f32[512]{0:T(512)S(1)}, ...), condition=%wide.region_15.16_spmd, body=%wide.region_11.15_spmd.sunk | while | flops 789187 | bytes 290481 | solution.py:43
  147.8 0.2 fusion.71
  148.0 0.6 fusion.72
  148.6 0.2 convolution_bitcast_fusion.12
  148.8 37.2 %all-reduce.5 = (f32[]{:T(128)}, f32[64]{0:T(128)S(1)}) all-reduce(f32[]{:T(128)} %get-tuple-element.478, f32[64]{0:T(128)S(1)} %convolution_bitcast_fusion.12), channel_id=1, replica_groups=mesh['tm'=16,'state'=2] {'tm'}, use_global_device_ids=true, to_apply=%region_13.13 | all-reduce | flops 65 | bytes 520 | tf_op jit(solution)/shard_map/while/body/eval_jaxpr/psum | solution.py:35
  186.9 0.2 fusion.71
  187.1 0.6 fusion.72
  187.7 0.2 convolution_bitcast_fusion.12
  187.9 39.2 %all-reduce.5 = (f32[]{:T(128)}, f32[64]{0:T(128)S(1)}) all-reduce(f32[]{:T(128)} %get-tuple-element.478, f32[64]{0:T(128)S(1)} %convolution_bitcast_fusion.12), channel_id=1, replica_groups=mesh['tm'=16,'state'=2] {'tm'}, use_global_device_ids=true, to_apply=%region_13.13 | all-reduce | flops 65 | bytes 520 | tf_op jit(solution)/shard_map/while/body/eval_jaxpr/psum | solution.py:35
  228.0 0.2 fusion.71
  228.2 0.6 fusion.72
  228.8 0.2 convolution_bitcast_fusion.12
  229.0 37.3 %all-reduce.5 = (f32[]{:T(128)}, f32[64]{0:T(128)S(1)}) all-reduce(f32[]{:T(128)} %get-tuple-element.478, f32[64]{0:T(128)S(1)} %convolution_bitcast_fusion.12), channel_id=1, replica_groups=mesh['tm'=16,'state'=2] {'tm'}, use_global_device_ids=true, to_apply=%region_13.13 | all-reduce | flops 65 | bytes 520 | tf_op jit(solution)/shard_map/while/body/eval_jaxpr/psum | solution.py:35
  267.1 0.2 fusion.71
  267.3 0.6 fusion.72
  267.9 0.2 convolution_bitcast_fusion.12
  268.1 39.2 %all-reduce.5 = (f32[]{:T(128)}, f32[64]{0:T(128)S(1)}) all-reduce(f32[]{:T(128)} %get-tuple-element.478, f32[64]{0:T(128)S(1)} %convolution_bitcast_fusion.12), channel_id=1, replica_groups=mesh['tm'=16,'state'=2] {'tm'}, use_global_device_ids=true, to_apply=%region_13.13 | all-reduce | flops 65 | bytes 520 | tf_op jit(solution)/shard_map/while/body/eval_jaxpr/psum | solution.py:35
  308.2 0.6 copy-done.5
  (76 shorter events, 2.0 us)
Async XLA Ops:
  7.2 1.2 copy-start
  7.2 92.1 %all-gather.2.cloned.1.call-start = ((), (), s32[]{:S(2)}) async-start(), calls=%async_computation | async-start | bytes 4456448 | tf_op jit(solution)/shard_map/all_gather | solution.py:11
  13.2 7.6 %copy-start.4 = (f32[512]{0:T(512)S(1)}, f32[512]{0:T(512)}, u32[]{:S(2)}) copy-start(f32[512]{0:T(512)} %param.17) | copy-start | bytes 6148
  13.2 8.2 %copy-start.1 = (f32[1,64,512]{2,1,0:T(8,128)S(1)}, f32[1,64,512]{2,1,0:T(8,128)}, u32[]{:S(2)}) copy-start(f32[1,64,512]{2,1,0:T(8,128)} %param.15) | copy-start | bytes 393220
  13.2 8.2 %copy-start.2 = (f32[1,64,512]{2,1,0:T(8,128)S(1)}, f32[1,64,512]{2,1,0:T(8,128)}, u32[]{:S(2)}) copy-start(f32[1,64,512]{2,1,0:T(8,128)} %param.16) | copy-start | bytes 393220
  101.8 46.0 %copy-start.3 = (f32[1,512]{1,0:T(1,128)S(1)}, f32[1,512]{1,0:T(1,128)}, u32[]{:S(2)}) copy-start(f32[1,512]{1,0:T(1,128)} %param.14) | copy-start | bytes 6148
  104.1 2.1 collective-permute-start
  308.2 0.6 copy-start.5
  308.2 0.6 copy-start.6
Sparse Core Ops, SparseCore 0:
  20.9 78.2 all-gather.1
